TPU v7x, 32 devices: a whole 2x2x4 slice. The times are simulated.
32 devices in a mesh: seg: 4 (over y, x), lat: 8 (over z, core).
Axes of the slice: x: 2, y: 2, z: 4, core: 2. Of those that a mesh axis runs over, the one named last changes fastest.
Arguments:
- coh_map: bfloat16 [4, 65536, 128], P('seg', 'lat'), may hold values from 0 to 40, as said below
- positions: int32 [4, 1024], P('seg', 'lat'), may hold values from 0 to 16776959, as said below
- counts: int32 [16], P('lat'), may hold values from 1 to 64, as said below
Outputs:
- semi_stat: bfloat16 [1024, 128], P('lat')
- excess: float32 [16, 128], P('lat')
Inputs may be any that keep to these rules, and one draw needn't show every extreme that they name: `coh_map`: nonnegative. `counts`: the first block has 1 valid point and the last block 64. `positions`: the bins are split into 8 aligned slices of 8192 bins; a point's two bins lie in the same slice; in each segment, at most 32 of the 128 points of one index of lat have their bins in one slice, and that most is reached in every draw.
All inputs are finite; a program needn't handle non-finite values.
Results may differ from a plain program's by a relative error of at most 0.001.
Values sent between devices are 32-bit elements; how exact they have to be, the bound alone decides.
A program may use at most 64 MiB of HBM per device.

v0:
```python
import jax
import jax.numpy as jnp
from jax import lax
from jax.sharding import PartitionSpec as P


def routed_sums(positions, coh_map, first_bin):
    seg_count = coh_map.shape[0]
    slice_bins = coh_map.shape[1]
    width = coh_map.shape[2]
    own_rows = positions.shape[1]
    n_lataxis = lax.axis_size("lat")
    slot_limit = 2 * own_rows // n_lataxis
    dest = positions // 256 // slice_bins
    dest_hits = (dest[:, :, None] == lax.broadcasted_iota(jnp.int32, (1, 1, n_lataxis), 2)).astype(
        jnp.int32
    )
    before = jnp.cumsum(dest_hits, axis=1) - dest_hits
    slot = jnp.sum(before * dest_hits, axis=2)
    seg_ids = lax.broadcasted_iota(jnp.int32, positions.shape, 0)
    outgoing = (
        jnp.full((n_lataxis, seg_count, slot_limit), -1, jnp.int32)
        .at[dest, seg_ids, slot]
        .set(positions)
    )
    bin_index = lax.broadcasted_iota(jnp.int32, (1, slice_bins), 1)
    incoming = lax.all_to_all(outgoing, "lat", split_axis=0, concat_axis=0, tiled=True)
    item_count = incoming.shape[2]
    pos_flat = incoming[:, 0, :].reshape(-1)
    live = (pos_flat >= 0)[:, None]
    rel_bin = (pos_flat // 256 - first_bin)[:, None]
    fraction = (pos_flat % 256).astype(jnp.float32)[:, None] / 256.0
    weights = jnp.where(live & (bin_index == rel_bin), 1.0 - fraction, 0.0) + jnp.where(
        live & (bin_index == rel_bin + 1), fraction, 0.0
    )
    rows = jnp.dot(weights.astype(jnp.bfloat16), coh_map[0], preferred_element_type=jnp.float32)
    row_list = [rows.reshape(n_lataxis, item_count, width)]
    stacked = jnp.stack(row_list, axis=1)
    returned = lax.all_to_all(stacked, "lat", split_axis=0, concat_axis=0, tiled=True)
    by_segment = returned.transpose(1, 0, 2, 3).reshape(seg_count, n_lataxis * slot_limit, width)
    flat_index = dest * slot_limit + slot
    picked = jnp.take_along_axis(by_segment, flat_index[:, :, None], axis=1)
    return jnp.sum(picked, axis=0)


def shards(coh_map, positions, counts):
    seg_count = coh_map.shape[0]
    slice_bins = coh_map.shape[1]
    first_bin = lax.axis_index("lat") * slice_bins
    n_segaxis = lax.axis_size("seg")
    total_segs = seg_count * n_segaxis
    own_rows = positions.shape[1]
    local_sums_rows = routed_sums(positions, coh_map, first_bin)
    summed = lax.psum(local_sums_rows, "seg")
    semi_stat = summed / total_segs
    block_count = counts.shape[0]
    block_size = own_rows // block_count
    grouped = semi_stat.reshape(block_count, block_size, semi_stat.shape[1])
    slot_index = lax.broadcasted_iota(jnp.int32, (block_count, block_size, 1), 1)
    live_mask = slot_index < counts[:, None, None]
    block_sums = jnp.sum(jnp.where(live_mask, grouped, 0.0), axis=1)
    count_float = counts.astype(jnp.float32)
    block_means = block_sums / count_float[:, None]
    column_sums, total_count = lax.psum((jnp.sum(block_sums, axis=0), jnp.sum(count_float)), "lat")
    global_mean = column_sums / total_count
    excess = block_means - global_mean[None, :]
    return (semi_stat.astype(jnp.bfloat16), excess)


def solution(mesh):
    in_specs = (P("seg", "lat", None), P("seg", "lat"), P("lat"))
    out_specs = (P("lat", None), P("lat", None))
    return jax.shard_map(shards, mesh=mesh, in_specs=in_specs, out_specs=out_specs, check_vma=False)
```

profile of v0, /device:TPU:0, one launch (start us, length us, event | category | flops | bytes accessed | tf_op | source)
XLA Modules:
  0.0 125.4 jit_solution(7126655053401794815)
XLA Ops:
  7.2 0.0 copy-start
  7.2 0.8 fusion.19
  8.0 0.1 fusion.12
  8.1 0.2 reduce_window_sum.11
  8.3 0.2 select_reduce_fusion.2
  8.5 0.6 broadcast.427
  9.1 19.9 %scatter_fusion = s32[8,32]{1,0:T(8,128)} fusion(s32[8,32]{1,0:T(8,128)} %broadcast.427, s32[128]{0:T(128)S(1)} %fusion.21, s32[128]{0:T(128)} %bitcast.50), kind=kCustom, calls=%fused_computation.1 | custom fusion | bytes 2560 | tf_op jit(solution)/shard_map/scatter | solution.py:24
  29.0 6.4 %all-to-all-start = ((s32[8,1,32]{2,1,0:T(1,128)}), s32[8,1,32]{2,1,0:T(1,128)S(1)}, u32[]{:S(2)}, u32[]{:S(2)}) async-start(s32[8,1,32]{2,1,0:T(1,128)} %bitcast.9), calls=%async_computation | async-start | bytes 8192 | tf_op jit(solution)/shard_map/all_to_all | solution.py:27
  35.3 0.7 iota_compare_fusion.3
  36.0 4.8 %all-to-all-done = s32[8,1,32]{2,1,0:T(1,128)S(1)} async-done(((s32[8,1,32]{2,1,0:T(1,128)}), s32[8,1,32]{2,1,0:T(1,128)S(1)}, u32[]{:S(2)}, u32[]{:S(2)}) %all-to-all-start) | async-done | bytes 1056 | tf_op jit(solution)/shard_map/all_to_all | solution.py:27
  40.9 0.0 copy-done
  40.9 0.0 copy-start.1
  40.9 5.0 %fusion.7 = f32[8,1,32,128]{3,2,1,0:T(8,128)} fusion(bf16[1,8192,128]{2,1,0:T(8,128)(2,1)S(1)} %copy-done, f32[8,32]{1,0:T(8,128)S(1)} %get-tuple-element.5, s32[8,32]{1,0:T(8,128)S(1)} %get-tuple-element.6, f32[8,32]{1,0:T(8,128)S(1)} %get-tuple-element.4, s32[8,32]{1,0:T(8,128)S(1)} %get-tuple-element.7, pred[8,32]{1,0:T(8,128)(4,1)S(1)} %broadcast_compare_fusion), kind=kOutput, calls=%fused_computation.11 | convolution fusion | flops 553648128 | bytes 2232576 | tf_op jit(solution)/shard_map/dot_general | solution.py:36
  45.9 3.4 %all-to-all-start.1 = ((f32[8,1,32,128]{3,2,1,0:T(8,128)}), f32[8,1,32,128]{3,2,1,0:T(8,128)S(1)}, u32[]{:S(2)}, u32[]{:S(2)}) async-start(f32[8,1,32,128]{3,2,1,0:T(8,128)} %fusion.7), calls=%async_computation.1 | async-start | bytes 262144 | tf_op jit(solution)/shard_map/all_to_all | solution.py:39
  49.2 0.0 all-reduce.3.cloned.1.call-start
  49.3 0.0 copy-done.1
  49.3 0.1 lt.77
  49.4 6.5 %all-to-all-done.1 = f32[8,1,32,128]{3,2,1,0:T(8,128)S(1)} async-done(((f32[8,1,32,128]{3,2,1,0:T(8,128)}), f32[8,1,32,128]{3,2,1,0:T(8,128)S(1)}, u32[]{:S(2)}, u32[]{:S(2)}) %all-to-all-start.1) | async-done | bytes 131104 | tf_op jit(solution)/shard_map/all_to_all | solution.py:39
  55.9 0.6 gather_fusion
  56.6 0.7 broadcast_select_fusion
  57.3 0.0 all-reduce.3.cloned.1.call-update
  57.3 0.6 convert_reduce_fusion
  57.9 40.4 %all-reduce.3.cloned.1.call-done = f32[128,128]{1,0:T(8,128)} async-done(((f32[128,128]{1,0:T(8,128)}), f32[128,128]{1,0:T(8,128)}) %all-reduce.3.cloned.1.call-update) | async-done | bytes 65552 | tf_op jit(solution)/shard_map/psum | solution.py:54
  98.3 1.5 %select_reduce_fusion = (f32[128]{0:T(128)S(1)}, bf16[128,128]{1,0:T(8,128)(2,1)}) fusion(pred[128]{0:T(512)(128)(4,1)S(1)} %lt.77, f32[128,128]{1,0:T(8,128)} %all-reduce.3.cloned.1.call-done), kind=kLoop, calls=%fused_computation.12 | loop fusion | flops 65408 | bytes 98944 | tf_op jit(solution)/shard_map/reduce_sum | solution.py:64
  99.8 16.6 %all-reduce = (f32[128]{0:T(128)S(1)}, f32[]{:T(128)}) all-reduce(f32[128]{0:T(128)S(1)} %get-tuple-element.10, f32[]{:T(128)} %convert_reduce_fusion), channel_id=1, replica_groups=mesh['seg'=4,'lat'=8] {'lat'}, use_global_device_ids=true, to_apply=%region_6.7 | all-reduce | flops 129 | bytes 1032 | tf_op jit(solution)/shard_map/psum | solution.py:64
  116.3 0.6 broadcast_divide_fusion
  117.0 0.9 select_reduce_fusion.1
  117.9 0.6 divide_subtract_fusion
  (11 shorter events, 0.1 us)
Async XLA Ops:
  7.2 33.7 %copy-start = (bf16[1,8192,128]{2,1,0:T(8,128)(2,1)S(1)}, bf16[1,8192,128]{2,1,0:T(8,128)(2,1)}, u32[]{:S(2)}) copy-start(bf16[1,8192,128]{2,1,0:T(8,128)(2,1)} %param.3) | copy-start | bytes 6291460
  29.0 11.9 %all-to-all-start = ((s32[8,1,32]{2,1,0:T(1,128)}), s32[8,1,32]{2,1,0:T(1,128)S(1)}, u32[]{:S(2)}, u32[]{:S(2)}) async-start(s32[8,1,32]{2,1,0:T(1,128)} %bitcast.9), calls=%async_computation | async-start | bytes 8192 | tf_op jit(solution)/shard_map/all_to_all | solution.py:27
  40.9 8.4 %copy-start.1 = (s32[2]{0:T(128)S(1)}, s32[2]{0:T(128)}, u32[]{:S(2)}) copy-start(s32[2]{0:T(128)} %param.5) | copy-start | bytes 28
  45.9 10.1 %all-to-all-start.1 = ((f32[8,1,32,128]{3,2,1,0:T(8,128)}), f32[8,1,32,128]{3,2,1,0:T(8,128)S(1)}, u32[]{:S(2)}, u32[]{:S(2)}) async-start(f32[8,1,32,128]{3,2,1,0:T(8,128)} %fusion.7), calls=%async_computation.1 | async-start | bytes 262144 | tf_op jit(solution)/shard_map/all_to_all | solution.py:39
  49.2 49.1 %all-reduce.3.cloned.1.call-start = ((), (), s32[]{:S(2)}) async-start(), calls=%async_computation.2 | async-start | bytes 131072 | tf_op jit(solution)/shard_map/psum | solution.py:54
Sparse Core Ops, SparseCore 0:
  57.4 40.8 all-reduce.2
where the time goes:
time: 126 us; the launch traced here: 125 us
  waiting for transfers between devices  51.7 us (41%)
  local copies, waits for them, and re-layouts  21.2 us (17%)
  blocking collectives  16.6 us (13%)
  between operations  14.1 us (11%)
  starting transfers between devices  9.76 us (8%)
  other arithmetic  7.05 us (6%)
  matrix products  4.96 us (4%)
    psum x1, waiting for transfers between devices, shards(): summed = lax.psum(local_sums_rows, 'seg')  40.4 us
    scatter x1, local copies, waits for them, and re-layouts, routed_sums(): outgoing = jnp.full((n_lataxis, seg_count, slot_limit), -1, jnp.int32).at...  19.9 us
    psum x1, blocking collectives, shards(): lax.psum((jnp.sum(block_sums, axis=0), jnp.sum(count_float)), 'lat')  16.6 us
    all_to_all x1, waiting for transfers between devices, routed_sums(): lax.all_to_all(stacked, 'lat', split_axis=0, concat_axis=0, tiled=True)  6.51 us
    all_to_all x1, starting transfers between devices, routed_sums(): lax.all_to_all(outgoing, 'lat', split_axis=0, concat_axis=0, tiled=True)  6.35 us
    dot_general x1, matrix products, routed_sums(): jnp.dot(weights.astype(jnp.bfloat16), coh_map[0], preferred_element_type=...  4.96 us
    all_to_all x1, waiting for transfers between devices, routed_sums(): lax.all_to_all(outgoing, 'lat', split_axis=0, concat_axis=0, tiled=True)  4.77 us
    all_to_all x1, starting transfers between devices, routed_sums(): lax.all_to_all(stacked, 'lat', split_axis=0, concat_axis=0, tiled=True)  3.37 us
  transfers between devices with their start and end apart: 3, of which 3 were waited for; matrix products, arithmetic and copies ran while one was open for 1% of the time, Pallas kernels for 0%

commit v1 on v0

--- a/solution.py
+++ b/solution.py
@@ -51,7 +51,7 @@
     total_segs = seg_count * n_segaxis
     own_rows = positions.shape[1]
     local_sums_rows = routed_sums(positions, coh_map, first_bin)
-    summed = lax.psum(local_sums_rows, "seg")
+    summed = jnp.sum(lax.all_gather(local_sums_rows, "seg"), axis=0)
     semi_stat = summed / total_segs
     block_count = counts.shape[0]
     block_size = own_rows // block_count

time: 126 us -> 76.1 us (0.60)
  waiting for transfers between devices: 51.7 us -> 10.7 us
  between operations: 14.1 us -> 0.75 us
  blocking collectives: 16.6 us -> 23.2 us
  other arithmetic: 7.05 us -> 4.77 us
    psum x1 -> x0, waiting for transfers between devices: 40.4 us -> none  [shards(): summed = lax.psum(local_sums_rows, 'seg')]
    all_gather x0 -> x1, blocking collectives: none -> 8.99 us  [shards(): summed = jnp.sum(lax.all_gather(local_sums_rows, 'seg'), axis=0)]
    psum x1, blocking collectives: 16.6 us -> 14.2 us  [shards(): lax.psum((jnp.sum(block_sums, axis=0), jnp.sum(count_float)), 'lat')]
  transfers between devices with their start and end apart: 3 -> 2, of which waited for: 3 -> 2; matrix products, arithmetic and copies ran while one was open for 1% -> 2% of each run, Pallas kernels for 0% -> 0%
where the time goes in v1:
time: 76.1 us; the launch traced here: 75.4 us
  blocking collectives  23.2 us (30%)
  local copies, waits for them, and re-layouts  21.2 us (28%)
  waiting for transfers between devices  10.7 us (14%)
  starting transfers between devices  9.72 us (13%)
  matrix products  4.96 us (7%)
  other arithmetic  4.77 us (6%)
    scatter x1, local copies, waits for them, and re-layouts, routed_sums(): outgoing = jnp.full((n_lataxis, seg_count, slot_limit), -1, jnp.int32).at...  19.9 us
    psum x1, blocking collectives, shards(): lax.psum((jnp.sum(block_sums, axis=0), jnp.sum(count_float)), 'lat')  14.2 us
    all_gather x1, blocking collectives, shards(): summed = jnp.sum(lax.all_gather(local_sums_rows, 'seg'), axis=0)  8.99 us
    all_to_all x1, starting transfers between devices, routed_sums(): lax.all_to_all(outgoing, 'lat', split_axis=0, concat_axis=0, tiled=True)  6.35 us
    all_to_all x1, waiting for transfers between devices, routed_sums(): lax.all_to_all(stacked, 'lat', split_axis=0, concat_axis=0, tiled=True)  5.98 us
    dot_general x1, matrix products, routed_sums(): jnp.dot(weights.astype(jnp.bfloat16), coh_map[0], preferred_element_type=...  4.96 us
    all_to_all x1, waiting for transfers between devices, routed_sums(): lax.all_to_all(outgoing, 'lat', split_axis=0, concat_axis=0, tiled=True)  4.77 us
    all_to_all x1, starting transfers between devices, routed_sums(): lax.all_to_all(stacked, 'lat', split_axis=0, concat_axis=0, tiled=True)  3.37 us
  transfers between devices with their start and end apart: 2, of which 2 were waited for; matrix products, arithmetic and copies ran while one was open for 2% of the time, Pallas kernels for 0%

profile of v1, /device:TPU:0, one launch (start us, length us, event | category | flops | bytes accessed | tf_op | source)
XLA Modules:
  0.0 75.4 jit_solution(15194445208628261132)
XLA Ops:
  0.6 0.0 copy-start
  0.6 0.8 %fusion.19 = (s32[1,128,1]{1,2,0:T(1,128)S(1)}, s32[1,128]{1,0:T(1,128)S(1)}) fusion(s32[1,128]{1,0:T(1,128)} %param.4), kind=kLoop, calls=%fused_computation.56 | loop fusion | flops 4224 | bytes 1536 | tf_op jit(solution)/shard_map/broadcast_in_dim | solution.py:24
  1.5 0.1 fusion.12
  1.6 0.2 reduce_window_sum.11
  1.7 0.2 select_reduce_fusion.2
  2.0 0.6 broadcast.449
  2.6 19.9 %scatter_fusion = s32[8,32]{1,0:T(8,128)} fusion(s32[8,32]{1,0:T(8,128)} %broadcast.449, s32[128]{0:T(128)S(1)} %fusion.21, s32[128]{0:T(128)} %bitcast.52), kind=kCustom, calls=%fused_computation.1 | custom fusion | bytes 2560 | tf_op jit(solution)/shard_map/scatter | solution.py:24
  22.4 6.4 %all-to-all-start = ((s32[8,1,32]{2,1,0:T(1,128)}), s32[8,1,32]{2,1,0:T(1,128)S(1)}, u32[]{:S(2)}, u32[]{:S(2)}) async-start(s32[8,1,32]{2,1,0:T(1,128)} %bitcast.9), calls=%async_computation | async-start | bytes 8192 | tf_op jit(solution)/shard_map/all_to_all | solution.py:27
  28.8 0.7 iota_compare_fusion.3
  29.5 4.8 %all-to-all-done = s32[8,1,32]{2,1,0:T(1,128)S(1)} async-done(((s32[8,1,32]{2,1,0:T(1,128)}), s32[8,1,32]{2,1,0:T(1,128)S(1)}, u32[]{:S(2)}, u32[]{:S(2)}) %all-to-all-start) | async-done | bytes 1056 | tf_op jit(solution)/shard_map/all_to_all | solution.py:27
  34.3 0.0 copy-done
  34.3 0.0 copy-start.1
  34.4 5.0 %fusion.7 = f32[8,1,32,128]{3,2,1,0:T(8,128)} fusion(bf16[1,8192,128]{2,1,0:T(8,128)(2,1)S(1)} %copy-done, f32[8,32]{1,0:T(8,128)S(1)} %get-tuple-element.5, s32[8,32]{1,0:T(8,128)S(1)} %get-tuple-element.6, f32[8,32]{1,0:T(8,128)S(1)} %get-tuple-element.4, s32[8,32]{1,0:T(8,128)S(1)} %get-tuple-element.7, pred[8,32]{1,0:T(8,128)(4,1)S(1)} %broadcast_compare_fusion), kind=kOutput, calls=%fused_computation.11 | convolution fusion | flops 553648128 | bytes 2232576 | tf_op jit(solution)/shard_map/dot_general | solution.py:36
  39.3 3.4 %all-to-all-start.1 = ((f32[8,1,32,128]{3,2,1,0:T(8,128)}), f32[8,1,32,128]{3,2,1,0:T(8,128)S(1)}, u32[]{:S(2)}, u32[]{:S(2)}) async-start(f32[8,1,32,128]{3,2,1,0:T(8,128)} %fusion.7), calls=%async_computation.1 | async-start | bytes 262144 | tf_op jit(solution)/shard_map/all_to_all | solution.py:39
  42.7 0.0 copy-done.1
  42.7 0.6 convert_reduce_fusion
  43.3 0.1 lt.77
  43.4 6.0 %all-to-all-done.1 = f32[8,1,32,128]{3,2,1,0:T(8,128)S(1)} async-done(((f32[8,1,32,128]{3,2,1,0:T(8,128)}), f32[8,1,32,128]{3,2,1,0:T(8,128)S(1)}, u32[]{:S(2)}, u32[]{:S(2)}) %all-to-all-start.1) | async-done | bytes 131104 | tf_op jit(solution)/shard_map/all_to_all | solution.py:39
  49.4 0.6 gather_fusion
  50.0 0.1 bitcast_select_fusion
  50.1 9.0 %all_gather.4 = f32[4,128,128]{2,1,0:T(8,128)S(1)} all-gather(f32[1,128,128]{2,1,0:T(8,128)S(1)} %bitcast_select_fusion), channel_id=1, replica_groups=mesh['seg'=4,'lat'=8] {'seg'}, dimensions={0}, use_global_device_ids=true | all-gather | bytes 327680 | tf_op jit(solution)/shard_map/all_gather | solution.py:54
  59.1 0.1 select_reduce_fusion.1
  59.2 0.6 select_reduce_fusion
  59.9 14.2 %all-reduce = (f32[128]{0:T(128)S(1)}, f32[]{:T(128)}) all-reduce(f32[128]{0:T(128)S(1)} %get-tuple-element.10, f32[]{:T(128)} %convert_reduce_fusion), channel_id=1, replica_groups=mesh['seg'=4,'lat'=8] {'lat'}, use_global_device_ids=true, to_apply=%region_6.7 | all-reduce | flops 129 | bytes 1032 | tf_op jit(solution)/shard_map/psum | solution.py:64
  74.1 0.6 broadcast_divide_fusion
  74.7 0.6 divide_subtract_fusion
  (12 shorter events, 0.1 us)
Async XLA Ops:
  0.6 33.7 %copy-start = (bf16[1,8192,128]{2,1,0:T(8,128)(2,1)S(1)}, bf16[1,8192,128]{2,1,0:T(8,128)(2,1)}, u32[]{:S(2)}) copy-start(bf16[1,8192,128]{2,1,0:T(8,128)(2,1)} %param.3) | copy-start | bytes 6291460
  22.4 11.9 %all-to-all-start = ((s32[8,1,32]{2,1,0:T(1,128)}), s32[8,1,32]{2,1,0:T(1,128)S(1)}, u32[]{:S(2)}, u32[]{:S(2)}) async-start(s32[8,1,32]{2,1,0:T(1,128)} %bitcast.9), calls=%async_computation | async-start | bytes 8192 | tf_op jit(solution)/shard_map/all_to_all | solution.py:27
  34.3 8.4 %copy-start.1 = (s32[2]{0:T(128)S(1)}, s32[2]{0:T(128)}, u32[]{:S(2)}) copy-start(s32[2]{0:T(128)} %param.5) | copy-start | bytes 28
  39.3 10.1 %all-to-all-start.1 = ((f32[8,1,32,128]{3,2,1,0:T(8,128)}), f32[8,1,32,128]{3,2,1,0:T(8,128)S(1)}, u32[]{:S(2)}, u32[]{:S(2)}) async-start(f32[8,1,32,128]{3,2,1,0:T(8,128)} %fusion.7), calls=%async_computation.1 | async-start | bytes 262144 | tf_op jit(solution)/shard_map/all_to_all | solution.py:39
